TPU v7x, 256 devices: a whole 4x4x8 slice. The times are simulated.
256 devices in a mesh: gx: 16 (over z, x_lo), gy: 16 (over y, x_hi, core).
Axes of the slice: x: 4 (x_hi: 2, x_lo: 2; x = x_hi * 2 + x_lo), y: 4, z: 8, core: 2. Of those that a mesh axis runs over, the one named last changes fastest.
Arguments:
- gradient: float32 [2048, 512], P('gx', 'gy'), may hold values from -6 to 6
- stat_old: float32 [2048, 2048], P('gx', 'gy'), may hold values from -1.001 to 1.001, as said below
Outputs:
- statistic: float32 [2048, 2048], P('gx', 'gy')
- inverse_root: float32 [2048, 2048], P('gx', 'gy')
Inputs may be any that keep to these rules, and one draw needn't show every extreme that they name: stat_old is symmetric positive semidefinite with unit diagonal, the Gram matrix of 2048 unit-length rows of 512 entries.
All inputs are finite; a program needn't handle non-finite values.
Results may differ from a plain program's by a relative error of at most 0.0003.
Values sent between devices are 32-bit elements.
A program may use at most 64 MiB of HBM per device.

v0:
```python
import jax
import jax.numpy as jnp
from jax import lax
from jax.sharding import Mesh
from jax.sharding import PartitionSpec as P

GY = ("gy_0", "gy_1", "gy_2")
GX = ("gx_0", "gx_1")
GX_GY = ("gx_0", "gx_1", "gy_0", "gy_1", "gy_2")


def gather_axes(array, axes, dim):
    filled = array
    for number in range(len(axes) - 1, -1, -1):
        filled = lax.all_gather(filled, axes[number], axis=dim, tiled=True)
    return filled


def folded(array, axes, dim, take_in, carry):
    everything = jax.tree.map(lambda part: gather_axes(part, axes, dim), array)
    return take_in(carry, everything, jnp.int32(0))


def spread(array, axes, root):
    array = jnp.where(lax.axis_index(axes) == root, array, jnp.zeros_like(array))
    for axis in axes:
        array = lax.psum(array, axis)
    return array


def over_axes(array, axes):
    for axis in axes:
        array = lax.psum(array, axis)
    return array


def matmul(leading, trailing):
    return jnp.dot(
        leading, trailing, preferred_element_type=jnp.float32, precision=lax.Precision.HIGHEST
    )


def panels(factor_one, factor_two):
    whole_row = lax.all_gather(factor_one, GY, axis=1, tiled=True)

    def accumulate(running, shard_rows, first_row):
        matching = lax.dynamic_slice_in_dim(whole_row, first_row, shard_rows.shape[0], 1)
        return running + matmul(matching, shard_rows)

    empty = jnp.zeros((factor_one.shape[0], factor_two.shape[1]), jnp.float32)
    return folded(factor_two, GX, 0, accumulate, empty)


def product(factor_one, factor_two):
    return panels(factor_one, factor_two)


def local(gradient, stat_old):
    count_rows = lax.axis_size(GX)
    count_cols = lax.axis_size(GY)
    factor = count_rows // count_cols
    piece_width = stat_old.shape[0]
    row_index = lax.axis_index(GX)
    col_index = lax.axis_index(GY)
    panel_rows = lax.all_gather(gradient, GY, axis=1, tiled=True)
    outer_parts = []
    for member in range(factor):
        column_rows = spread(panel_rows, GX, col_index * factor + member)
        outer_parts.append(matmul(panel_rows, column_rows.T))
    outer = jnp.concatenate(outer_parts, axis=1) / panel_rows.shape[1]
    statistic = 0.9 * stat_old + outer
    squares = over_axes(jnp.sum(statistic * statistic), GX_GY)
    divisor = 2.0 * jnp.sqrt(squares / (piece_width * count_rows))
    global_rows = row_index * piece_width + lax.broadcasted_iota(jnp.int32, stat_old.shape, 0)
    global_cols = col_index * (factor * piece_width) + lax.broadcasted_iota(
        jnp.int32, stat_old.shape, 1
    )
    identity = (global_rows == global_cols).astype(jnp.float32)
    normed = statistic / divisor
    first_step = 1.5 * identity - 0.5 * normed
    root_half = product(normed, first_step)
    product_mid = product(first_step, root_half)
    second_step = 1.5 * identity - 0.5 * product_mid
    inverse_root = product(second_step, first_step)
    return (statistic, inverse_root)


def solution(mesh):
    torus = Mesh(mesh.devices.reshape(8, 2, 4, 2, 2), ("gx_0", "gx_1", "gy_0", "gy_1", "gy_2"))
    placed = (P(GX, GY), P(GX, GY))
    return jax.shard_map(
        local, mesh=torus, in_specs=placed, out_specs=(P(GX, GY), P(GX, GY)), check_vma=False
    )
```

profile of v0, /device:TPU:1, one launch (start us, length us, event | category | flops | bytes accessed | tf_op | source)
XLA Modules:
  0.0 435.5 jit_solution(8363940582427046131)
XLA Ops:
  7.2 0.0 copy-start.3
  7.2 0.0 all-reduce.3.cloned.1.call-start
  7.2 0.7 copy-done.3
  7.9 26.8 %all_gather.26 = f32[128,512]{0,1:T(8,128)S(1)} all-gather(f32[128,32]{0,1:T(8,128)S(1)} %copy-done.3), channel_id=1, replica_groups=mesh['gx_0'=8,'gx_1'=2,'gy_0'=4,'gy_1'=2,'gy_2'=2] {'gy_0','gy_1','gy_2'}, dimensions={1}, use_global_device_ids=true | all-gather | bytes 278528 | tf_op jit(solution)/shard_map/all_gather | solution.py:65
  34.6 0.7 broadcast_select_fusion
  35.4 0.0 all-reduce.3.cloned.1.call-update
  35.4 0.0 all-reduce.5.cloned.1.call-start
  35.4 65.4 %all-reduce.3.cloned.1.call-done = f32[128,512]{0,1:T(8,128)} async-done(((f32[128,512]{0,1:T(8,128)}), f32[128,512]{0,1:T(8,128)}) %all-reduce.3.cloned.1.call-update) | async-done | bytes 262160 | tf_op jit(solution)/shard_map/psum | solution.py:27
  100.8 0.0 copy-start.2
  100.8 0.0 all-reduce.5.cloned.1.call-update
  100.8 0.0 all-gather.10.cloned.1.call-start
  100.9 0.8 copy-done.2
  101.6 0.1 copy.4
  101.7 39.7 %all-reduce.5.cloned.1.call-done = f32[128,512]{0,1:T(8,128)} async-done(((f32[128,512]{0,1:T(8,128)}), f32[128,512]{0,1:T(8,128)}) %all-reduce.5.cloned.1.call-update) | async-done | bytes 262160 | tf_op jit(solution)/shard_map/psum | solution.py:27
  141.4 2.1 multiply_reduce_fusion
  143.6 14.6 %psum.51 = f32[]{:T(128)} all-reduce(f32[]{:T(128)} %get-tuple-element.6), channel_id=1, replica_groups=mesh['gx_0'=8,'gx_1'=2,'gy_0'=4,'gy_1'=2,'gy_2'=2] {'gx_0'}, use_global_device_ids=true, to_apply=%region_3.4 | all-reduce | flops 1 | bytes 8 | tf_op jit(solution)/shard_map/psum | solution.py:33
  158.1 4.4 %psum.52 = f32[]{:T(128)} all-reduce(f32[]{:T(128)} %psum.51), channel_id=1, replica_groups=mesh['gx_0'=8,'gx_1'=2,'gy_0'=4,'gy_1'=2,'gy_2'=2] {'gx_1'}, use_global_device_ids=true, to_apply=%region_4.5 | all-reduce | flops 1 | bytes 8 | tf_op jit(solution)/shard_map/psum | solution.py:33
  162.5 9.1 %psum.53 = f32[]{:T(128)} all-reduce(f32[]{:T(128)} %psum.52), channel_id=1, replica_groups=mesh['gx_0'=8,'gx_1'=2,'gy_0'=4,'gy_1'=2,'gy_2'=2] {'gy_0'}, use_global_device_ids=true, to_apply=%region_5.6 | all-reduce | flops 1 | bytes 8 | tf_op jit(solution)/shard_map/psum | solution.py:33
  171.6 5.9 %psum.54 = f32[]{:T(128)} all-reduce(f32[]{:T(128)} %psum.53), channel_id=1, replica_groups=mesh['gx_0'=8,'gx_1'=2,'gy_0'=4,'gy_1'=2,'gy_2'=2] {'gy_1'}, use_global_device_ids=true, to_apply=%region_6.7 | all-reduce | flops 1 | bytes 8 | tf_op jit(solution)/shard_map/psum | solution.py:33
  177.5 11.8 %psum.55 = f32[]{:T(128)} all-reduce(f32[]{:T(128)} %psum.54), channel_id=1, replica_groups=mesh['gx_0'=8,'gx_1'=2,'gy_0'=4,'gy_1'=2,'gy_2'=2] {'gy_2'}, use_global_device_ids=true, to_apply=%region_7.8 | all-reduce | flops 1 | bytes 8 | tf_op jit(solution)/shard_map/psum | solution.py:33
  190.0 0.6 select_subtract_fusion
  190.6 0.0 copy-start.1
  190.6 3.9 all_gather.29
  194.5 0.0 copy-done.1
  194.5 0.0 all-gather.10.cloned.1.call-update
  194.5 0.0 all-gather.8.cloned.1.call-start
  194.6 0.5 all-gather.8.cloned.1.call-update
  195.1 0.0 all-gather.6.cloned.1.call-start
  195.1 0.5 all-gather.6.cloned.1.call-update
  195.7 0.0 all-gather.12.cloned.1.call-start
  195.7 29.4 %all-gather.10.cloned.1.call-done = f32[2048,128]{0,1:T(8,128)} async-done(((f32[256,128]{0,1:T(8,128)}), f32[2048,128]{0,1:T(8,128)}) %all-gather.10.cloned.1.call-update) | async-done | bytes 1048592 | tf_op jit(solution)/shard_map/all_gather | solution.py:15
  225.1 56.8 %all-gather.8.cloned.1.call-done = f32[128,2048]{0,1:T(8,128)} async-done(((f32[128,128]{0,1:T(8,128)}), f32[128,2048]{0,1:T(8,128)}) %all-gather.8.cloned.1.call-update) | async-done | bytes 1048592 | tf_op jit(solution)/shard_map/all_gather | solution.py:44
  281.9 3.4 fusion.3
  285.2 3.9 all_gather.31
  289.1 0.0 all-gather.12.cloned.1.call-update
  289.1 0.0 copy-start
  289.1 0.0 all-gather.14.cloned.1.call-start
  289.2 44.5 %all-gather.6.cloned.1.call-done = f32[128,2048]{0,1:T(8,128)} async-done(((f32[128,128]{0,1:T(8,128)}), f32[128,2048]{0,1:T(8,128)}) %all-gather.6.cloned.1.call-update) | async-done | bytes 1048592 | tf_op jit(solution)/shard_map/all_gather | solution.py:44
  333.7 33.6 %all-gather.12.cloned.1.call-done = f32[2048,128]{1,0:T(8,128)} async-done(((f32[256,128]{1,0:T(8,128)}), f32[2048,128]{1,0:T(8,128)}) %all-gather.12.cloned.1.call-update) | async-done | bytes 1048592 | tf_op jit(solution)/shard_map/all_gather | solution.py:15
  367.3 4.0 fusion
  371.3 0.0 all-gather.14.cloned.1.call-update
  371.3 0.7 copy.5
  372.0 53.0 %all-gather.14.cloned.1.call-done = f32[128,2048]{0,1:T(8,128)} async-done(((f32[128,128]{0,1:T(8,128)}), f32[128,2048]{0,1:T(8,128)}) %all-gather.14.cloned.1.call-update) | async-done | bytes 1048592 | tf_op jit(solution)/shard_map/all_gather | solution.py:44
  425.0 0.0 copy-done
  425.0 3.7 fusion.4
  (1 shorter events, 0.0 us)
Async XLA Ops:
  7.2 0.7 copy-start.3
  7.2 93.6 %all-reduce.3.cloned.1.call-start = ((), (), s32[]{:S(2)}) async-start(), calls=%async_computation | async-start | bytes 524288 | tf_op jit(solution)/shard_map/psum | solution.py:27
  35.4 106.1 %all-reduce.5.cloned.1.call-start = ((), (), s32[]{:S(2)}) async-start(), calls=%async_computation.1 | async-start | bytes 524288 | tf_op jit(solution)/shard_map/psum | solution.py:27
  100.8 0.8 copy-start.2
  100.8 124.2 %all-gather.10.cloned.1.call-start = ((), (), s32[]{:S(2)}) async-start(), calls=%async_computation.4 | async-start | bytes 1179648 | tf_op jit(solution)/shard_map/all_gather | solution.py:15
  190.6 3.9 copy-start.1
  194.5 87.3 %all-gather.8.cloned.1.call-start = ((), (), s32[]{:S(2)}) async-start(), calls=%async_computation.3 | async-start | bytes 1114112 | tf_op jit(solution)/shard_map/all_gather | solution.py:44
  195.1 138.6 %all-gather.6.cloned.1.call-start = ((), (), s32[]{:S(2)}) async-start(), calls=%async_computation.2 | async-start | bytes 1114112 | tf_op jit(solution)/shard_map/all_gather | solution.py:44
  195.7 171.6 %all-gather.12.cloned.1.call-start = ((), (), s32[]{:S(2)}) async-start(), calls=%async_computation.5 | async-start | bytes 1179648 | tf_op jit(solution)/shard_map/all_gather | solution.py:15
  289.1 135.9 %copy-start = (f32[2048,128]{0,1:T(8,128)S(1)}, f32[2048,128]{0,1:T(8,128)}, u32[]{:S(2)}) copy-start(f32[2048,128]{0,1:T(8,128)} %all-gather.10.cloned.1.call-done) | copy-start | bytes 3145732
  289.1 135.9 %all-gather.14.cloned.1.call-start = ((), (), s32[]{:S(2)}) async-start(), calls=%async_computation.6 | async-start | bytes 1114112 | tf_op jit(solution)/shard_map/all_gather | solution.py:44
Sparse Core Ops, SparseCore 0:
  35.5 65.2 all-reduce.2
  103.4 38.0 all-reduce.4
  194.6 30.4 all-gather.9
  228.3 53.5 all-gather.7
  285.0 48.6 all-gather.5
  335.4 31.8 all-gather.11
  371.4 53.5 all-gather.13
where the time goes:
time: 436 us
  waiting for transfers between devices  323 us (74%)
  blocking collectives  80.2 us (18%)
  between operations  14.9 us (3%)
  matrix products  13.2 us (3%)
    all_gather x3, waiting for transfers between devices, panels(): whole_row = lax.all_gather(factor_one, GY, axis=1, tiled=True)  154 us
    psum x2, waiting for transfers between devices, spread(): array = lax.psum(array, axis)  105 us
    all_gather x2, waiting for transfers between devices, gather_axes(): filled = lax.all_gather(filled, axes[number], axis=dim, tiled=True)  62.9 us
    psum x5, blocking collectives, over_axes(): array = lax.psum(array, axis)  45.7 us
    all_gather x1, blocking collectives, local(): panel_rows = lax.all_gather(gradient, GY, axis=1, tiled=True)  26.8 us
    dot_general x4, matrix products, matmul(): jnp.dot(leading, trailing, preferred_element_type=jnp.float32, precision=...  13.2 us
  transfers between devices with their start and end apart: 7, of which 7 were waited for; matrix products, arithmetic and copies ran while one was open for 1% of the time, Pallas kernels for 0%

commit v1 on v0

--- a/solution.py
+++ b/solution.py
@@ -24,7 +24,7 @@
 def spread(array, axes, root):
     array = jnp.where(lax.axis_index(axes) == root, array, jnp.zeros_like(array))
     for axis in axes:
-        array = lax.psum(array, axis)
+        array = jnp.sum(lax.all_gather(array, axis), axis=0)
     return array
 
 

time: 436 us -> 382 us (0.88)
  waiting for transfers between devices: 323 us -> 258 us
  blocking collectives: 80.2 us -> 90.6 us
    psum x2 -> x0, waiting for transfers between devices: 105 us -> none  [spread(): array = lax.psum(array, axis)]
    all_gather x0 -> x1, waiting for transfers between devices: none -> 39.5 us  [spread(): array = jnp.sum(lax.all_gather(array, axis), axis=0)]
    all_gather x0 -> x1, blocking collectives: none -> 5.89 us  [spread(): array = jnp.sum(lax.all_gather(array, axis), axis=0)]
  transfers between devices with their start and end apart: 7 -> 6, of which waited for: 7 -> 6; matrix products, arithmetic and copies ran while one was open for 1% -> 1% of each run, Pallas kernels for 0% -> 0%
where the time goes in v1:
time: 382 us
  waiting for transfers between devices  258 us (68%)
  blocking collectives  90.6 us (24%)
  between operations  14.9 us (4%)
  matrix products  12.2 us (3%)
  local copies, waits for them, and re-layouts  3.99 us (1%)
    all_gather x3, waiting for transfers between devices, panels(): whole_row = lax.all_gather(factor_one, GY, axis=1, tiled=True)  154 us
    all_gather x2, waiting for transfers between devices, gather_axes(): filled = lax.all_gather(filled, axes[number], axis=dim, tiled=True)  62.4 us
    psum x5, blocking collectives, over_axes(): array = lax.psum(array, axis)  49.9 us
    all_gather x1, waiting for transfers between devices, spread(): array = jnp.sum(lax.all_gather(array, axis), axis=0)  39.5 us
    all_gather x1, blocking collectives, local(): panel_rows = lax.all_gather(gradient, GY, axis=1, tiled=True)  27 us
    dot_general x4, matrix products, matmul(): jnp.dot(leading, trailing, preferred_element_type=jnp.float32, precision=...  12.2 us
    all_gather x2, blocking collectives, gather_axes(): filled = lax.all_gather(filled, axes[number], axis=dim, tiled=True)  7.76 us
  transfers between devices with their start and end apart: 6, of which 6 were waited for; matrix products, arithmetic and copies ran while one was open for 1% of the time, Pallas kernels for 0%

profile of v1, /device:TPU:1, one launch (start us, length us, event | category | flops | bytes accessed | tf_op | source)
XLA Modules:
  0.0 382.0 jit_solution(9099397590832761059)
XLA Ops:
  7.2 0.0 all-gather.19.cloned.1.call-start
  7.2 27.0 %all_gather.38 = f32[128,512]{0,1:T(8,128)S(1)} all-gather(f32[128,32]{0,1:T(8,128)} %param.2), channel_id=1, replica_groups=mesh['gx_0'=8,'gx_1'=2,'gy_0'=4,'gy_1'=2,'gy_2'=2] {'gy_0','gy_1','gy_2'}, dimensions={1}, use_global_device_ids=true | all-gather | bytes 278528 | tf_op jit(solution)/shard_map/all_gather | solution.py:65
  34.2 0.7 broadcast_select_fusion
  35.0 0.0 all-gather.19.cloned.1.call-update
  35.0 0.0 all-gather.13.cloned.1.call-start
  35.0 0.9 copy.8
  36.0 39.5 %all-gather.19.cloned.1.call-done = f32[1024,512]{0,1:T(8,128)} async-done(((f32[128,512]{0,1:T(8,128)}), f32[1024,512]{0,1:T(8,128)}) %all-gather.19.cloned.1.call-update) | async-done | bytes 2097168 | tf_op jit(solution)/shard_map/all_gather | solution.py:27
  75.5 2.1 copy.12
  77.5 0.6 bitcast_reduce_fusion
  78.1 5.9 %all-gather.1 = f32[256,512]{0,1:T(8,128)S(1)} all-gather(f32[128,512]{0,1:T(8,128)S(1)} %bitcast_reduce_fusion), channel_id=3, replica_groups=mesh['gx_0'=8,'gx_1'=2,'gy_0'=4,'gy_1'=2,'gy_2'=2] {'gx_1'}, dimensions={0}, use_global_device_ids=true | all-gather | bytes 786432 | tf_op jit(solution)/shard_map/all_gather | solution.py:27
  84.0 0.3 reshape.5
  84.3 0.6 reduce_sum.28
  84.9 1.2 multiply_reduce_fusion
  86.1 13.3 %psum.35 = f32[]{:T(128)} all-reduce(f32[]{:T(128)} %get-tuple-element.10), channel_id=1, replica_groups=mesh['gx_0'=8,'gx_1'=2,'gy_0'=4,'gy_1'=2,'gy_2'=2] {'gx_0'}, use_global_device_ids=true, to_apply=%region_3.4 | all-reduce | flops 1 | bytes 8 | tf_op jit(solution)/shard_map/psum | solution.py:33
  99.3 4.4 %psum.36 = f32[]{:T(128)} all-reduce(f32[]{:T(128)} %psum.35), channel_id=1, replica_groups=mesh['gx_0'=8,'gx_1'=2,'gy_0'=4,'gy_1'=2,'gy_2'=2] {'gx_1'}, use_global_device_ids=true, to_apply=%region_4.5 | all-reduce | flops 1 | bytes 8 | tf_op jit(solution)/shard_map/psum | solution.py:33
  103.7 9.4 %psum.37 = f32[]{:T(128)} all-reduce(f32[]{:T(128)} %psum.36), channel_id=1, replica_groups=mesh['gx_0'=8,'gx_1'=2,'gy_0'=4,'gy_1'=2,'gy_2'=2] {'gy_0'}, use_global_device_ids=true, to_apply=%region_5.6 | all-reduce | flops 1 | bytes 8 | tf_op jit(solution)/shard_map/psum | solution.py:33
  113.1 5.9 %psum.38 = f32[]{:T(128)} all-reduce(f32[]{:T(128)} %psum.37), channel_id=1, replica_groups=mesh['gx_0'=8,'gx_1'=2,'gy_0'=4,'gy_1'=2,'gy_2'=2] {'gy_1'}, use_global_device_ids=true, to_apply=%region_6.7 | all-reduce | flops 1 | bytes 8 | tf_op jit(solution)/shard_map/psum | solution.py:33
  119.0 17.1 %psum.39 = f32[]{:T(128)} all-reduce(f32[]{:T(128)} %psum.38), channel_id=1, replica_groups=mesh['gx_0'=8,'gx_1'=2,'gy_0'=4,'gy_1'=2,'gy_2'=2] {'gy_2'}, use_global_device_ids=true, to_apply=%region_7.8 | all-reduce | flops 1 | bytes 8 | tf_op jit(solution)/shard_map/psum | solution.py:33
  136.7 0.6 select_subtract_fusion
  137.4 0.0 copy-start.1
  137.4 3.9 %all_gather.45 = f32[256,128]{0,1:T(8,128)} all-gather(f32[128,128]{0,1:T(8,128)S(1)} %get-tuple-element.8), channel_id=1, replica_groups=mesh['gx_0'=8,'gx_1'=2,'gy_0'=4,'gy_1'=2,'gy_2'=2] {'gx_1'}, dimensions={0}, use_global_device_ids=true | all-gather | bytes 196608 | tf_op jit(solution)/shard_map/all_gather | solution.py:15
  141.2 0.0 all-gather.13.cloned.1.call-update
  141.3 0.0 all-gather.11.cloned.1.call-start
  141.3 0.7 all-gather.11.cloned.1.call-update
  142.0 0.0 all-gather.9.cloned.1.call-start
  142.0 0.0 copy-done.1
  142.1 0.5 all-gather.9.cloned.1.call-update
  142.6 0.0 all-gather.15.cloned.1.call-start
  142.6 28.8 %all-gather.13.cloned.1.call-done = f32[2048,128]{0,1:T(8,128)} async-done(((f32[256,128]{0,1:T(8,128)}), f32[2048,128]{0,1:T(8,128)}) %all-gather.13.cloned.1.call-update) | async-done | bytes 1048592 | tf_op jit(solution)/shard_map/all_gather | solution.py:15
  171.4 0.0 copy-start
  171.4 56.9 %all-gather.11.cloned.1.call-done = f32[128,2048]{0,1:T(8,128)} async-done(((f32[128,128]{0,1:T(8,128)}), f32[128,2048]{0,1:T(8,128)}) %all-gather.11.cloned.1.call-update) | async-done | bytes 1048592 | tf_op jit(solution)/shard_map/all_gather | solution.py:44
  228.4 3.4 fusion.3
  231.7 3.9 %all_gather.47 = f32[256,128]{1,0:T(8,128)} all-gather(f32[128,128]{1,0:T(8,128)S(1)} %fusion.3), channel_id=1, replica_groups=mesh['gx_0'=8,'gx_1'=2,'gy_0'=4,'gy_1'=2,'gy_2'=2] {'gx_1'}, dimensions={0}, use_global_device_ids=true | all-gather | bytes 196608 | tf_op jit(solution)/shard_map/all_gather | solution.py:15
  235.6 0.0 all-gather.15.cloned.1.call-update
  235.6 0.0 all-gather.17.cloned.1.call-start
  235.7 44.5 %all-gather.9.cloned.1.call-done = f32[128,2048]{0,1:T(8,128)} async-done(((f32[128,128]{0,1:T(8,128)}), f32[128,2048]{0,1:T(8,128)}) %all-gather.9.cloned.1.call-update) | async-done | bytes 1048592 | tf_op jit(solution)/shard_map/all_gather | solution.py:44
  280.2 33.6 %all-gather.15.cloned.1.call-done = f32[2048,128]{1,0:T(8,128)} async-done(((f32[256,128]{1,0:T(8,128)}), f32[2048,128]{1,0:T(8,128)}) %all-gather.15.cloned.1.call-update) | async-done | bytes 1048592 | tf_op jit(solution)/shard_map/all_gather | solution.py:15
  313.8 4.0 %fusion = f32[128,128]{0,1:T(8,128)} fusion(f32[128,2048]{0,1:T(8,128)} %all-gather.9.cloned.1.call-done, f32[2048,128]{1,0:T(8,128)} %all-gather.15.cloned.1.call-done, s32[128]{0:T(128)S(1)} %get-tuple-element.13, s32[128]{0:T(128)S(1)} %get-tuple-element.12), kind=kOutput, calls=%fused_computation.2 | convolution fusion | flops 402718720 | bytes 2163712 | tf_op jit(solution)/shard_map/dot_general | solution.py:38
  317.8 0.0 all-gather.17.cloned.1.call-update
  317.8 0.7 copy.10
  318.5 53.0 %all-gather.17.cloned.1.call-done = f32[128,2048]{0,1:T(8,128)} async-done(((f32[128,128]{0,1:T(8,128)}), f32[128,2048]{0,1:T(8,128)}) %all-gather.17.cloned.1.call-update) | async-done | bytes 1048592 | tf_op jit(solution)/shard_map/all_gather | solution.py:44
  371.5 0.0 copy-done
  371.5 3.7 fusion.4
  (1 shorter events, 0.0 us)
Async XLA Ops:
  7.2 68.3 %all-gather.19.cloned.1.call-start = ((), (), s32[]{:S(2)}) async-start(), calls=%async_computation.5 | async-start | bytes 2359296 | tf_op jit(solution)/shard_map/all_gather | solution.py:27
  35.0 136.4 %all-gather.13.cloned.1.call-start = ((), (), s32[]{:S(2)}) async-start(), calls=%async_computation.2 | async-start | bytes 1179648 | tf_op jit(solution)/shard_map/all_gather | solution.py:15
  137.4 4.7 %copy-start.1 = (f32[128,128]{0,1:T(8,128)}, f32[128,128]{0,1:T(8,128)S(1)}, u32[]{:S(2)}) copy-start(f32[128,128]{0,1:T(8,128)S(1)} %get-tuple-element.8) | copy-start | bytes 196612
  141.3 87.1 %all-gather.11.cloned.1.call-start = ((), (), s32[]{:S(2)}) async-start(), calls=%async_computation.1 | async-start | bytes 1114112 | tf_op jit(solution)/shard_map/all_gather | solution.py:44
  142.0 138.2 %all-gather.9.cloned.1.call-start = ((), (), s32[]{:S(2)}) async-start(), calls=%async_computation | async-start | bytes 1114112 | tf_op jit(solution)/shard_map/all_gather | solution.py:44
  142.6 171.2 %all-gather.15.cloned.1.call-start = ((), (), s32[]{:S(2)}) async-start(), calls=%async_computation.3 | async-start | bytes 1179648 | tf_op jit(solution)/shard_map/all_gather | solution.py:15
  171.4 200.1 %copy-start = (f32[2048,128]{0,1:T(8,128)S(1)}, f32[2048,128]{0,1:T(8,128)}, u32[]{:S(2)}) copy-start(f32[2048,128]{0,1:T(8,128)} %all-gather.13.cloned.1.call-done) | copy-start | bytes 3145732
  235.6 135.9 %all-gather.17.cloned.1.call-start = ((), (), s32[]{:S(2)}) async-start(), calls=%async_computation.4 | async-start | bytes 1114112 | tf_op jit(solution)/shard_map/all_gather | solution.py:44
Sparse Core Ops, SparseCore 0:
  35.1 40.3 all-gather.18
  141.4 29.9 all-gather.12
  174.8 53.5 all-gather.10
  231.5 48.6 all-gather.8
  281.9 31.8 all-gather.14
  317.9 53.5 all-gather.16
